TPU v7x, 32 devices: a whole 2x2x4 slice. The times are simulated.
32 devices in a mesh: owner: 4 (over y, core), rows: 8 (over z, x).
Axes of the slice: x: 2, y: 2, z: 4, core: 2. Of those that a mesh axis runs over, the one named last changes fastest.
Arguments:
- train_gate: float32 [128, 2048, 768], P('owner', 'rows'), may hold values from -0.125 to 0.125
- train_up: float32 [128, 2048, 768], P('owner', 'rows'), may hold values from -0.125 to 0.125
- router_weight: float32 [2048, 128], P('rows', 'owner'), may hold values from -0.125 to 0.125
- router_gain: float32 [2048], P('rows'), may hold values from 0.25 to 1.75
Outputs:
- ready_gate: bfloat16 [128, 768, 2048], P(('owner', 'rows'))
- ready_up: bfloat16 [128, 768, 2048], P(('owner', 'rows'))
- serve_router: bfloat16 [2048, 128], replicated
All inputs are finite; a program needn't handle non-finite values.
Results may differ from a plain program's by a relative error of at most 0.001.
Values may be sent and summed in bfloat16 or wider, within the bound.
A program may use at most 192 MiB of HBM per device.

v0:
```python
import jax
import jax.numpy as jnp
from jax import lax
from jax.sharding import PartitionSpec as P


def on_device(train_gate, train_up, router_weight, router_gain):
    narrow_gate, narrow_up = (train_gate.astype(jnp.bfloat16), train_up.astype(jnp.bfloat16))
    ready_gate, ready_up = (
        lax.all_to_all(narrow_gate, "rows", split_axis=0, concat_axis=1, tiled=True),
        lax.all_to_all(narrow_up, "rows", split_axis=0, concat_axis=1, tiled=True),
    )
    ready_gate = jnp.transpose(ready_gate, (0, 2, 1))
    ready_up = jnp.transpose(ready_up, (0, 2, 1))
    part_router = (router_weight * router_gain[:, None]).astype(jnp.bfloat16)
    row_router = lax.all_gather(part_router, "rows", axis=0, tiled=True)
    serve_router = lax.all_gather(row_router, "owner", axis=1, tiled=True)
    return (ready_gate, ready_up, serve_router)


def solution(mesh):
    placed = (P("owner", "rows", None), P("owner", "rows", None), P("rows", "owner"), P("rows"))
    return jax.shard_map(
        on_device,
        mesh=mesh,
        in_specs=placed,
        out_specs=(P(("owner", "rows"), None, None), P(("owner", "rows"), None, None), P()),
        check_vma=False,
    )
```

profile of v0, /device:TPU:0, one launch (start us, length us, event | category | flops | bytes accessed | tf_op | source)
XLA Modules:
  0.0 672.7 jit_solution(13268045616997217038)
XLA Ops:
  0.6 13.2 %convert_element_type.9 = bf16[32,256,768]{2,1,0:T(8,128)(2,1)} convert(f32[32,256,768]{2,1,0:T(8,128)} %param.4) | non-fusion elementwise | flops 6291456 | bytes 37748736 | tf_op jit(solution)/shard_map/convert_element_type | solution.py:8
  13.8 7.3 %all-to-all-start = ((bf16[32,256,768]{2,1,0:T(8,128)(2,1)}), bf16[32,256,768]{2,1,0:T(8,128)(2,1)}, u32[]{:S(2)}, u32[]{:S(2)}) async-start(bf16[32,256,768]{2,1,0:T(8,128)(2,1)} %convert_element_type.9), calls=%async_computation | async-start | bytes 25165824 | tf_op jit(solution)/shard_map/all_to_all | solution.py:10
  21.1 13.4 %convert_element_type.10 = bf16[32,256,768]{2,1,0:T(8,128)(2,1)} convert(f32[32,256,768]{2,1,0:T(8,128)} %param.5) | non-fusion elementwise | flops 6291456 | bytes 37748736 | tf_op jit(solution)/shard_map/convert_element_type | solution.py:8
  34.5 0.0 copy-start
  34.5 0.0 copy-start.1
  34.5 259.7 %all-to-all-done = bf16[32,256,768]{2,1,0:T(8,128)(2,1)} async-done(((bf16[32,256,768]{2,1,0:T(8,128)(2,1)}), bf16[32,256,768]{2,1,0:T(8,128)(2,1)}, u32[]{:S(2)}, u32[]{:S(2)}) %all-to-all-start) | async-done | bytes 12582944 | tf_op jit(solution)/shard_map/all_to_all | solution.py:10
  294.2 5.3 all-to-all-start.1
  299.5 0.0 copy-done
  299.5 0.0 copy-done.1
  299.5 292.2 %all_gather.6 = bf16[2048,32]{0,1:T(8,128)(2,1)S(1)} all-gather(bf16[256,32]{0,1:T(8,128)(2,1)S(1)} %multiply_convert_fusion), channel_id=1, replica_groups=mesh['owner'=4,'rows'=8] {'rows'}, dimensions={0}, use_global_device_ids=true | all-gather | bytes 147456 | tf_op jit(solution)/shard_map/all_gather | solution.py:16
  591.8 7.2 %all_gather.7 = bf16[2048,128]{0,1:T(8,128)(2,1)S(1)} all-gather(bf16[2048,32]{0,1:T(8,128)(2,1)S(1)} %all_gather.6), channel_id=1, replica_groups=mesh['owner'=4,'rows'=8] {'owner'}, dimensions={1}, use_global_device_ids=true | all-gather | bytes 655360 | tf_op jit(solution)/shard_map/all_gather | solution.py:17
  598.9 1.0 copy.12
  599.9 16.9 %copy.10 = bf16[8,4,256,768]{2,0,3,1:T(8,128)(2,1)} copy(bf16[8,4,256,768]{3,2,1,0:T(8,128)(2,1)} %bitcast) | data formatting | bytes 25165824 | tf_op jit(solution)/shard_map/all_to_all | solution.py:10
  616.8 19.5 %all_to_all.29 = bf16[4,2048,768]{1,2,0:T(8,128)(2,1)} reshape(bf16[4,8,256,768]{2,1,3,0:T(8,128)(2,1)} %bitcast.14) | data formatting | bytes 25165824 | tf_op jit(solution)/shard_map/all_to_all | solution.py:10
  636.3 0.0 all-to-all-done.1
  636.3 16.9 %copy.11 = bf16[8,4,256,768]{2,0,3,1:T(8,128)(2,1)} copy(bf16[8,4,256,768]{3,2,1,0:T(8,128)(2,1)} %bitcast.3) | data formatting | bytes 25165824 | tf_op jit(solution)/shard_map/all_to_all | solution.py:11
  653.2 19.5 %all_to_all.33 = bf16[4,2048,768]{1,2,0:T(8,128)(2,1)} reshape(bf16[4,8,256,768]{2,1,3,0:T(8,128)(2,1)} %bitcast.15) | data formatting | bytes 25165824 | tf_op jit(solution)/shard_map/all_to_all | solution.py:11
  (1 shorter events, 0.0 us)
Async XLA Ops:
  13.8 280.3 %all-to-all-start = ((bf16[32,256,768]{2,1,0:T(8,128)(2,1)}), bf16[32,256,768]{2,1,0:T(8,128)(2,1)}, u32[]{:S(2)}, u32[]{:S(2)}) async-start(bf16[32,256,768]{2,1,0:T(8,128)(2,1)} %convert_element_type.9), calls=%async_computation | async-start | bytes 25165824 | tf_op jit(solution)/shard_map/all_to_all | solution.py:10
  34.5 265.0 %copy-start = (f32[256,32]{0,1:T(8,128)S(1)}, f32[256,32]{0,1:T(8,128)}, u32[]{:S(2)}) copy-start(f32[256,32]{0,1:T(8,128)} %param.6) | copy-start | bytes 98308
  34.5 265.0 %copy-start.1 = (f32[256]{0:T(256)S(1)}, f32[256]{0:T(256)}, u32[]{:S(2)}) copy-start(f32[256]{0:T(256)} %param.7) | copy-start | bytes 3076
  294.2 342.1 %all-to-all-start.1 = ((bf16[32,256,768]{2,1,0:T(8,128)(2,1)}), bf16[32,256,768]{2,1,0:T(8,128)(2,1)}, u32[]{:S(2)}, u32[]{:S(2)}) async-start(bf16[32,256,768]{2,1,0:T(8,128)(2,1)} %convert_element_type.10), calls=%async_computation.1 | async-start | bytes 25165824 | tf_op jit(solution)/shard_map/all_to_all | solution.py:11
where the time goes:
time: 675 us; the launch traced here: 673 us
  blocking collectives  299 us (44%)
  waiting for transfers between devices  260 us (39%)
  local copies, waits for them, and re-layouts  73.7 us (11%)
  other arithmetic  26.6 us (4%)
  starting transfers between devices  12.6 us (2%)
    all_gather x1, blocking collectives, on_device(): row_router = lax.all_gather(part_router, 'rows', axis=0, tiled=True)  292 us
    all_to_all x1, waiting for transfers between devices, on_device(): lax.all_to_all(narrow_gate, 'rows', split_axis=0, concat_axis=1, tiled=True)  260 us
    all_to_all x2, local copies, waits for them, and re-layouts, on_device(): lax.all_to_all(narrow_up, 'rows', split_axis=0, concat_axis=1, tiled=True)  36.4 us
    all_to_all x2, local copies, waits for them, and re-layouts, on_device(): lax.all_to_all(narrow_gate, 'rows', split_axis=0, concat_axis=1, tiled=True)  36.3 us
  transfers between devices with their start and end apart: 2, of which 1 were waited for; matrix products, arithmetic and copies ran while one was open for 5% of the time, Pallas kernels for 0%

commit v1 on v0

--- a/solution.py
+++ b/solution.py
@@ -13,7 +13,16 @@
     ready_gate = jnp.transpose(ready_gate, (0, 2, 1))
     ready_up = jnp.transpose(ready_up, (0, 2, 1))
     part_router = (router_weight * router_gain[:, None]).astype(jnp.bfloat16)
-    row_router = lax.all_gather(part_router, "rows", axis=0, tiled=True)
+    ways = lax.axis_size("rows")
+    up = [(d, (d + 1) % ways) for d in range(ways)]
+    down = [(d, (d - 1) % ways) for d in range(ways)]
+    earlier, later = ([part_router], [part_router])
+    for _ in range(ways // 2):
+        earlier.append(lax.ppermute(earlier[-1], "rows", up))
+    for _ in range((ways - 1) // 2):
+        later.append(lax.ppermute(later[-1], "rows", down))
+    line = jnp.concatenate([*earlier[::-1], *later[1:]], axis=0)
+    row_router = jnp.roll(line, (lax.axis_index("rows") - ways // 2) * part_router.shape[0], axis=0)
     serve_router = lax.all_gather(row_router, "owner", axis=1, tiled=True)
     return (ready_gate, ready_up, serve_router)
 

time: 675 us -> 668 us (0.990)
  blocking collectives: 299 us -> 7.2 us
  waiting for transfers between devices: 260 us -> 474 us
  starting transfers between devices: 12.6 us -> 80.9 us
    all_gather x1 -> x0, blocking collectives: 292 us -> none  [on_device(): row_router = lax.all_gather(part_router, 'rows', axis=0, tiled=True)]
    ppermute x0 -> x7, waiting for transfers between devices: none -> 214 us  [the longest x4 209 us: on_device(): earlier.append(lax.ppermute(earlier[-1], 'rows', up))]
    ppermute x0 -> x7, starting transfers between devices: none -> 68.3 us  [the longest x4 59.4 us: on_device(): earlier.append(lax.ppermute(earlier[-1], 'rows', up))]
  transfers between devices with their start and end apart: 2 -> 9, of which waited for: 1 -> 7; matrix products, arithmetic and copies ran while one was open for 5% -> 5% of each run, Pallas kernels for 0% -> 0%
where the time goes in v1:
time: 668 us; the launch traced here: 663 us
  waiting for transfers between devices  474 us (71%)
  starting transfers between devices  80.9 us (12%)
  local copies, waits for them, and re-layouts  73.8 us (11%)
  other arithmetic  26.5 us (4%)
  blocking collectives  7.2 us (1%)
    all_to_all x1, waiting for transfers between devices, on_device(): lax.all_to_all(narrow_gate, 'rows', split_axis=0, concat_axis=1, tiled=True)  260 us
    ppermute x4, waiting for transfers between devices, on_device(): earlier.append(lax.ppermute(earlier[-1], 'rows', up))  209 us
    ppermute x4, starting transfers between devices, on_device(): earlier.append(lax.ppermute(earlier[-1], 'rows', up))  59.4 us
    all_to_all x2, local copies, waits for them, and re-layouts, on_device(): lax.all_to_all(narrow_up, 'rows', split_axis=0, concat_axis=1, tiled=True)  36.4 us
    all_to_all x2, local copies, waits for them, and re-layouts, on_device(): lax.all_to_all(narrow_gate, 'rows', split_axis=0, concat_axis=1, tiled=True)  36.3 us
  transfers between devices with their start and end apart: 9, of which 7 were waited for; matrix products, arithmetic and copies ran while one was open for 5% of the time, Pallas kernels for 0%

profile of v1, /device:TPU:0, one launch (start us, length us, event | category | flops | bytes accessed | tf_op | source)
XLA Modules:
  0.0 663.0 jit_solution(4247206100921887915)
XLA Ops:
  0.6 13.2 %convert_element_type.9 = bf16[32,256,768]{2,1,0:T(8,128)(2,1)} convert(f32[32,256,768]{2,1,0:T(8,128)} %param.4) | non-fusion elementwise | flops 6291456 | bytes 37748736 | tf_op jit(solution)/shard_map/convert_element_type | solution.py:8
  13.8 7.3 %all-to-all-start = ((bf16[32,256,768]{2,1,0:T(8,128)(2,1)}), bf16[32,256,768]{2,1,0:T(8,128)(2,1)}, u32[]{:S(2)}, u32[]{:S(2)}) async-start(bf16[32,256,768]{2,1,0:T(8,128)(2,1)} %convert_element_type.9), calls=%async_computation | async-start | bytes 25165824 | tf_op jit(solution)/shard_map/all_to_all | solution.py:10
  21.1 13.3 %convert_element_type.10 = bf16[32,256,768]{2,1,0:T(8,128)(2,1)} convert(f32[32,256,768]{2,1,0:T(8,128)} %param.5) | non-fusion elementwise | flops 6291456 | bytes 37748736 | tf_op jit(solution)/shard_map/convert_element_type | solution.py:8
  34.4 259.8 %all-to-all-done = bf16[32,256,768]{2,1,0:T(8,128)(2,1)} async-done(((bf16[32,256,768]{2,1,0:T(8,128)(2,1)}), bf16[32,256,768]{2,1,0:T(8,128)(2,1)}, u32[]{:S(2)}, u32[]{:S(2)}) %all-to-all-start) | async-done | bytes 12582944 | tf_op jit(solution)/shard_map/all_to_all | solution.py:10
  294.2 5.4 all-to-all-start.1
  299.6 1.9 collective-permute-start
  301.5 205.0 %collective-permute-done = bf16[256,32]{0,1:T(8,128)(2,1)S(1)} collective-permute-done((bf16[256,32]{0,1:T(8,128)(2,1)S(1)}, bf16[256,32]{0,1:T(8,128)(2,1)S(1)}, u32[]{:S(2)}, u32[]{:S(2)}) %collective-permute-start) | collective-permute-done | bytes 16416 | tf_op jit(solution)/shard_map/ppermute | solution.py:21
  506.5 0.0 collective-permute-start.1
  506.5 4.7 collective-permute-start.4
  511.2 1.8 collective-permute-done.1
  513.0 24.6 %collective-permute-start.2 = (bf16[256,32]{0,1:T(8,128)(2,1)S(1)}, bf16[256,32]{0,1:T(8,128)(2,1)S(1)}, u32[]{:S(2)}, u32[]{:S(2)}) collective-permute-start(bf16[256,32]{0,1:T(8,128)(2,1)S(1)} %collective-permute-done.1), channel_id=1, source_target_pairs={{0,1},{1,2},{2,3},{3,4},{4,5},{5,6},{6,7},{7,0},{8,9},{9,10},{10,1... | collective-permute-start | bytes 49160 | tf_op jit(solution)/shard_map/ppermute | solution.py:21
  537.6 0.0 collective-permute-done.4
  537.6 4.2 collective-permute-start.5
  541.8 1.7 collective-permute-done.2
  543.5 32.8 %collective-permute-start.3 = (bf16[256,32]{0,1:T(8,128)(2,1)S(1)}, bf16[256,32]{0,1:T(8,128)(2,1)S(1)}, u32[]{:S(2)}, u32[]{:S(2)}) collective-permute-start(bf16[256,32]{0,1:T(8,128)(2,1)S(1)} %collective-permute-done.2), channel_id=1, source_target_pairs={{0,1},{1,2},{2,3},{3,4},{4,5},{5,6},{6,7},{7,0},{8,9},{9,10},{10,1... | collective-permute-start | bytes 49160 | tf_op jit(solution)/shard_map/ppermute | solution.py:21
  576.4 0.5 collective-permute-done.5
  576.9 0.9 collective-permute-done.3
  577.8 4.1 collective-permute-done.6
  582.1 7.2 %all_gather.3 = bf16[2048,128]{0,1:T(8,128)(2,1)S(1)} all-gather(bf16[2048,32]{0,1:T(8,128)(2,1)S(1)} %constant_dynamic-slice_fusion), channel_id=1, replica_groups=mesh['owner'=4,'rows'=8] {'owner'}, dimensions={1}, use_global_device_ids=true | all-gather | bytes 655360 | tf_op jit(solution)/shard_map/all_gather | solution.py:26
  589.3 1.0 copy.12
  590.3 16.9 %copy.10 = bf16[8,4,256,768]{2,0,3,1:T(8,128)(2,1)} copy(bf16[8,4,256,768]{3,2,1,0:T(8,128)(2,1)} %bitcast) | data formatting | bytes 25165824 | tf_op jit(solution)/shard_map/all_to_all | solution.py:10
  607.2 19.5 %all_to_all.29 = bf16[4,2048,768]{1,2,0:T(8,128)(2,1)} reshape(bf16[4,8,256,768]{2,1,3,0:T(8,128)(2,1)} %bitcast.14) | data formatting | bytes 25165824 | tf_op jit(solution)/shard_map/all_to_all | solution.py:10
  626.7 16.9 %copy.11 = bf16[8,4,256,768]{2,0,3,1:T(8,128)(2,1)} copy(bf16[8,4,256,768]{3,2,1,0:T(8,128)(2,1)} %bitcast.3) | data formatting | bytes 25165824 | tf_op jit(solution)/shard_map/all_to_all | solution.py:11
  643.5 19.5 %all_to_all.33 = bf16[4,2048,768]{1,2,0:T(8,128)(2,1)} reshape(bf16[4,8,256,768]{2,1,3,0:T(8,128)(2,1)} %bitcast.15) | data formatting | bytes 25165824 | tf_op jit(solution)/shard_map/all_to_all | solution.py:11
  (24 shorter events, 0.1 us)
Async XLA Ops:
  13.8 280.3 %all-to-all-start = ((bf16[32,256,768]{2,1,0:T(8,128)(2,1)}), bf16[32,256,768]{2,1,0:T(8,128)(2,1)}, u32[]{:S(2)}, u32[]{:S(2)}) async-start(bf16[32,256,768]{2,1,0:T(8,128)(2,1)} %convert_element_type.9), calls=%async_computation | async-start | bytes 25165824 | tf_op jit(solution)/shard_map/all_to_all | solution.py:10
  34.4 265.2 %copy-start = (f32[256,32]{0,1:T(8,128)S(1)}, f32[256,32]{0,1:T(8,128)}, u32[]{:S(2)}) copy-start(f32[256,32]{0,1:T(8,128)} %param.6) | copy-start | bytes 98308
  34.4 265.2 %copy-start.1 = (f32[256]{0:T(256)S(1)}, f32[256]{0:T(256)}, u32[]{:S(2)}) copy-start(f32[256]{0:T(256)} %param.7) | copy-start | bytes 3076
  294.2 332.5 %all-to-all-start.1 = ((bf16[32,256,768]{2,1,0:T(8,128)(2,1)}), bf16[32,256,768]{2,1,0:T(8,128)(2,1)}, u32[]{:S(2)}, u32[]{:S(2)}) async-start(bf16[32,256,768]{2,1,0:T(8,128)(2,1)} %convert_element_type.10), calls=%async_computation.1 | async-start | bytes 25165824 | tf_op jit(solution)/shard_map/all_to_all | solution.py:11
  299.6 206.9 %collective-permute-start = (bf16[256,32]{0,1:T(8,128)(2,1)S(1)}, bf16[256,32]{0,1:T(8,128)(2,1)S(1)}, u32[]{:S(2)}, u32[]{:S(2)}) collective-permute-start(bf16[256,32]{0,1:T(8,128)(2,1)S(1)} %multiply_convert_fusion), channel_id=1, source_target_pairs={{0,1},{1,2},{2,3},{3,4},{4,5},{5,6},{6,7},{7,0},{8,9},{9,10},{10,1... | collective-permute-start | bytes 49160 | tf_op jit(solution)/shard_map/ppermute | solution.py:21
  506.5 6.5 collective-permute-start.1
  506.5 31.1 %collective-permute-start.4 = (bf16[256,32]{0,1:T(8,128)(2,1)S(1)}, bf16[256,32]{0,1:T(8,128)(2,1)S(1)}, u32[]{:S(2)}, u32[]{:S(2)}) collective-permute-start(bf16[256,32]{0,1:T(8,128)(2,1)S(1)} %multiply_convert_fusion), channel_id=1, source_target_pairs={{0,7},{1,0},{2,1},{3,2},{4,3},{5,4},{6,5},{7,6},{8,15},{9,8},{10,9... | collective-permute-start | bytes 49160 | tf_op jit(solution)/shard_map/ppermute | solution.py:23
  513.0 30.5 %collective-permute-start.2 = (bf16[256,32]{0,1:T(8,128)(2,1)S(1)}, bf16[256,32]{0,1:T(8,128)(2,1)S(1)}, u32[]{:S(2)}, u32[]{:S(2)}) collective-permute-start(bf16[256,32]{0,1:T(8,128)(2,1)S(1)} %collective-permute-done.1), channel_id=1, source_target_pairs={{0,1},{1,2},{2,3},{3,4},{4,5},{5,6},{6,7},{7,0},{8,9},{9,10},{10,1... | collective-permute-start | bytes 49160 | tf_op jit(solution)/shard_map/ppermute | solution.py:21
  537.6 39.3 %collective-permute-start.5 = (bf16[256,32]{0,1:T(8,128)(2,1)S(1)}, bf16[256,32]{0,1:T(8,128)(2,1)S(1)}, u32[]{:S(2)}, u32[]{:S(2)}) collective-permute-start(bf16[256,32]{0,1:T(8,128)(2,1)S(1)} %collective-permute-done.4), channel_id=1, source_target_pairs={{0,7},{1,0},{2,1},{3,2},{4,3},{5,4},{6,5},{7,6},{8,15},{9,8},{10,9... | collective-permute-start | bytes 49160 | tf_op jit(solution)/shard_map/ppermute | solution.py:23
  543.5 34.3 %collective-permute-start.3 = (bf16[256,32]{0,1:T(8,128)(2,1)S(1)}, bf16[256,32]{0,1:T(8,128)(2,1)S(1)}, u32[]{:S(2)}, u32[]{:S(2)}) collective-permute-start(bf16[256,32]{0,1:T(8,128)(2,1)S(1)} %collective-permute-done.2), channel_id=1, source_target_pairs={{0,1},{1,2},{2,3},{3,4},{4,5},{5,6},{6,7},{7,0},{8,9},{9,10},{10,1... | collective-permute-start | bytes 49160 | tf_op jit(solution)/shard_map/ppermute | solution.py:21
  576.9 5.1 collective-permute-start.6
